TPU v7x, 32 devices: a whole 2x2x4 slice. The times are simulated.
32 devices in a mesh: dp: 2 (over y), tensor: 4 (over x, core), ctx: 4 (over z).
Axes of the slice: x: 2, y: 2, z: 4, core: 2. Of those that a mesh axis runs over, the one named last changes fastest.
Arguments:
- grad_down: bfloat16 [2, 18432, 4608], P('dp', 'tensor', 'ctx'), may hold values from -700 to 700
- grad_query: bfloat16 [2, 4608, 2048], P('dp', 'ctx', 'tensor'), may hold values from -700 to 700
- down_param: float32 [18432, 4608], P(('tensor', 'dp'), 'ctx'), may hold values from -0.3 to 0.3
- down_moment: float32 [18432, 4608], P(('tensor', 'dp'), 'ctx'), may hold values from -6 to 6
- down_second: float32 [4608], P('ctx'), may hold values from 0.1 to 2
- query_param: float32 [4608, 2048], P(('ctx', 'dp'), 'tensor'), may hold values from -0.3 to 0.3
- query_moment: float32 [4608, 2048], P(('ctx', 'dp'), 'tensor'), may hold values from -6 to 6
- query_second: float32 [16], P('tensor'), may hold values from 0.1 to 2
- step_count: int32 [1], replicated, may hold values from 1 to 29
Outputs:
- down_param_new: float32 [18432, 4608], P(('tensor', 'dp'), 'ctx')
- down_moment_new: float32 [18432, 4608], P(('tensor', 'dp'), 'ctx')
- down_second_new: float32 [4608], P('ctx')
- down_update: bfloat16 [18432, 4608], P(('tensor', 'dp'), 'ctx')
- query_param_new: float32 [4608, 2048], P(('ctx', 'dp'), 'tensor')
- query_moment_new: float32 [4608, 2048], P(('ctx', 'dp'), 'tensor')
- query_second_new: float32 [16], P('tensor')
- query_update: bfloat16 [4608, 2048], P(('ctx', 'dp'), 'tensor')
All inputs are finite; a program needn't handle non-finite values.
Results may differ from a plain program's by a relative error of at most 0.012.
Values may be sent and summed in bfloat16 or wider, within the bound.
A program may use at most 128 MiB of HBM per device.

v0:
```python
import jax
import jax.numpy as jnp
from jax import lax
from jax.sharding import PartitionSpec as P

D = 4608
HEAD_DIM = 128
FF = 18432


BETA_ONE = 0.9
BETA_TWO = 0.95
EPSILON = 1e-08
LEARN_RATE = 0.003
DECAY_RATE = 0.1


def finish(parameter, moment, gradient, second_wide, keep_one, keep_two):
    moment_new = BETA_ONE * moment + (1.0 - BETA_ONE) * gradient
    update = moment_new / keep_one / (jnp.sqrt(second_wide / keep_two) + EPSILON)
    parameter_new = parameter - LEARN_RATE * (update + DECAY_RATE * parameter)
    return (parameter_new, moment_new, update.astype(jnp.bfloat16))


def shards(
    grad_down,
    grad_query,
    down_param,
    down_moment,
    down_second,
    query_param,
    query_moment,
    query_second,
    step_count,
):
    replicas = lax.axis_size("dp")
    step_value = step_count[0].astype(jnp.float32)
    keep_one = 1.0 - jnp.power(jnp.float32(BETA_ONE), step_value)
    keep_two = 1.0 - jnp.power(jnp.float32(BETA_TWO), step_value)
    down_summed, query_summed = (
        lax.psum_scatter(grad_down[0], "dp", scatter_dimension=0, tiled=True).astype(jnp.float32),
        lax.psum_scatter(grad_query[0], "dp", scatter_dimension=0, tiled=True).astype(jnp.float32),
    )
    down_grad = down_summed / replicas
    neuron_part = jnp.sum(down_grad * down_grad, axis=0)
    query_grad = query_summed / replicas
    head_count = query_grad.shape[1] // HEAD_DIM
    head_part = jnp.sum(
        (query_grad * query_grad).reshape(query_grad.shape[0], head_count, HEAD_DIM), axis=(0, 2)
    )
    neuron_total = lax.psum(neuron_part, ("dp", "tensor"))
    head_total = lax.psum(head_part, ("dp", "ctx"))
    down_second_new = BETA_TWO * down_second + (1.0 - BETA_TWO) * (neuron_total / FF)
    query_second_new = BETA_TWO * query_second + (1.0 - BETA_TWO) * (head_total / (D * HEAD_DIM))
    down_param_new, down_moment_new, down_update = finish(
        down_param, down_moment, down_grad, down_second_new[None, :], keep_one, keep_two
    )
    query_wide = jnp.repeat(query_second_new, HEAD_DIM)
    query_param_new, query_moment_new, query_update = finish(
        query_param, query_moment, query_grad, query_wide[None, :], keep_one, keep_two
    )
    return (
        down_param_new,
        down_moment_new,
        down_second_new,
        down_update,
        query_param_new,
        query_moment_new,
        query_second_new,
        query_update,
    )


def solution(mesh):
    in_specs = (
        P("dp", "tensor", "ctx"),
        P("dp", "ctx", "tensor"),
        P(("tensor", "dp"), "ctx"),
        P(("tensor", "dp"), "ctx"),
        P("ctx"),
        P(("ctx", "dp"), "tensor"),
        P(("ctx", "dp"), "tensor"),
        P("tensor"),
        P(),
    )
    out_specs = (
        P(("tensor", "dp"), "ctx"),
        P(("tensor", "dp"), "ctx"),
        P("ctx"),
        P(("tensor", "dp"), "ctx"),
        P(("ctx", "dp"), "tensor"),
        P(("ctx", "dp"), "tensor"),
        P("tensor"),
        P(("ctx", "dp"), "tensor"),
    )
    return jax.shard_map(shards, mesh=mesh, in_specs=in_specs, out_specs=out_specs, check_vma=False)
```

profile of v0, /device:TPU:0, one launch (start us, length us, event | category | flops | bytes accessed | tf_op | source)
XLA Modules:
  0.0 202.6 jit_solution(13049623929021003127)
XLA Ops:
  7.2 0.0 reduce-scatter.5.cloned.1.call-start
  7.2 0.7 reduce-scatter.5.cloned.1.call-update
  7.9 0.0 reduce-scatter.3.cloned.1.call-start
  7.9 0.0 copy-start.4
  8.0 0.0 copy-start.2
  8.0 0.7 reduce-scatter.3.cloned.1.call-update
  9.4 25.4 %reduce-scatter.5.cloned.1.call-done = bf16[576,512]{1,0:T(8,128)(2,1)} async-done(((bf16[1152,512]{1,0:T(8,128)(2,1)}), bf16[576,512]{1,0:T(8,128)(2,1)}) %reduce-scatter.5.cloned.1.call-update) | async-done | bytes 589840 | tf_op jit(solution)/shard_map/reduce_scatter | solution.py:42
  34.8 1.3 fusion.6
  36.1 0.1 bitcast_reduce_fusion
  36.2 20.8 %psum.15 = f32[4]{0:T(128)S(1)} all-reduce(f32[4]{0:T(128)S(1)} %bitcast_reduce_fusion), channel_id=1, replica_groups=mesh['dp'=2,'tensor'=4,'ctx'=4] {'dp','ctx'}, use_global_device_ids=true, to_apply=%region_6.7 | all-reduce | flops 4 | bytes 32 | tf_op jit(solution)/shard_map/psum | solution.py:52
  57.0 0.0 copy-done.4
  57.0 0.5 add_multiply_fusion.1
  57.5 0.1 broadcast_bitcast_fusion
  57.6 0.0 copy-done.2
  57.6 2.1 %fusion.7 = (bf16[576,512]{1,0:T(8,128)(2,1)}, f32[576,512]{1,0:T(8,128)S(1)}) fusion(f32[512]{0:T(512)S(1)} %broadcast_bitcast_fusion, bf16[576,512]{1,0:T(8,128)(2,1)} %reduce-scatter.5.cloned.1.call-done, f32[576,512]{1,0:T(8,128)S(1)} %copy-done.2), kind=kLoop, calls=%fused_computation.15 | loop fusion | flops 1769472 | bytes 3540992 | tf_op jit(solution)/shard_map/convert_element_type | solution.py:22
  59.7 3.0 %multiply_subtract_fusion.1 = f32[576,512]{1,0:T(8,128)} fusion(f32[576,512]{1,0:T(8,128)} %param.14, f32[576,512]{1,0:T(8,128)S(1)} %get-tuple-element.9, f32[512]{0:T(512)S(1)} %broadcast_bitcast_fusion), kind=kLoop, calls=%fused_computation.13 | loop fusion | flops 1474560 | bytes 3540992 | tf_op jit(solution)/shard_map/sub | solution.py:21
  62.7 98.0 %reduce-scatter.3.cloned.1.call-done = bf16[2304,1152]{1,0:T(8,128)(2,1)} async-done(((bf16[4608,1152]{1,0:T(8,128)(2,1)}), bf16[2304,1152]{1,0:T(8,128)(2,1)}) %reduce-scatter.3.cloned.1.call-update) | async-done | bytes 5308432 | tf_op jit(solution)/shard_map/reduce_scatter | solution.py:41
  160.8 4.1 %fusion.2 = f32[1152]{0:T(1024)S(1)} fusion(bf16[2304,1152]{1,0:T(8,128)(2,1)} %reduce-scatter.3.cloned.1.call-done), kind=kLoop, calls=%fused_computation.4 | loop fusion | flops 10615680 | bytes 5313024 | tf_op jit(solution)/shard_map/reduce_sum | solution.py:45
  164.9 12.8 %psum.14 = f32[1152]{0:T(1024)S(1)} all-reduce(f32[1152]{0:T(1024)S(1)} %fusion.2), channel_id=1, replica_groups=mesh['dp'=2,'tensor'=4,'ctx'=4] {'dp','tensor'}, use_global_device_ids=true, to_apply=%region_2.0 | all-reduce | flops 1152 | bytes 9216 | tf_op jit(solution)/shard_map/psum | solution.py:51
  177.6 0.0 copy-done.3
  177.6 0.6 add_multiply_fusion
  178.3 10.2 %fusion.3 = (bf16[2304,1152]{1,0:T(8,128)(2,1)}, f32[2304,1152]{1,0:T(8,128)S(1)}) fusion(f32[1152]{0:T(1024)S(1)} %get-tuple-element.14, bf16[2304,1152]{1,0:T(8,128)(2,1)} %reduce-scatter.3.cloned.1.call-done, f32[2304,1152]{1,0:T(8,128)} %param.12), kind=kLoop, calls=%fused_computation.7 | loop fusion | flops 15925248 | bytes 31855104 | tf_op jit(solution)/shard_map/convert_element_type | solution.py:22
  188.5 6.2 %multiply_subtract_fusion = f32[2304,1152]{1,0:T(8,128)} fusion(f32[2304,1152]{1,0:T(8,128)S(1)} %bitcast.10, f32[2304,1152]{1,0:T(8,128)S(1)} %get-tuple-element.13, f32[1152]{0:T(1024)S(1)} %get-tuple-element.14), kind=kLoop, calls=%fused_computation.5 | loop fusion | flops 13271040 | bytes 31855104 | tf_op jit(solution)/shard_map/sub | solution.py:21
  194.7 1.1 copy-done
  (11 shorter events, 0.0 us)
Async XLA Ops:
  7.2 27.6 %reduce-scatter.5.cloned.1.call-start = ((), (), s32[]{:S(2)}) async-start(), calls=%async_computation.3 | async-start | bytes 1769472 | tf_op jit(solution)/shard_map/reduce_scatter | solution.py:42
  7.9 152.9 %reduce-scatter.3.cloned.1.call-start = ((), (), s32[]{:S(2)}) async-start(), calls=%async_computation.2 | async-start | bytes 15925248 | tf_op jit(solution)/shard_map/reduce_scatter | solution.py:41
  7.9 49.1 %copy-start.4 = (f32[4]{0:T(128)S(1)}, f32[4]{0:T(128)}, u32[]{:S(2)}) copy-start(f32[4]{0:T(128)} %param.16) | copy-start | bytes 52
  8.0 49.6 %copy-start.2 = (f32[576,512]{1,0:T(8,128)S(1)}, f32[576,512]{1,0:T(8,128)}, u32[]{:S(2)}) copy-start(f32[576,512]{1,0:T(8,128)} %param.15) | copy-start | bytes 3538948
  59.7 128.7 %copy-start.1 = (f32[576,512]{1,0:T(8,128)}, f32[576,512]{1,0:T(8,128)S(1)}, u32[]{:S(2)}) copy-start(f32[576,512]{1,0:T(8,128)S(1)} %get-tuple-element.9) | copy-start | bytes 3538948
  59.7 117.9 %copy-start.3 = (f32[1152]{0:T(1024)S(1)}, f32[1152]{0:T(1024)}, u32[]{:S(2)}) copy-start(f32[1152]{0:T(1024)} %param.13) | copy-start | bytes 13828
  160.8 27.7 %slice-start = ((s8[10616832]{0:T(1024)(128)(4,1)}), s8[2228224]{0:T(1024)(128)(4,1)S(1)}, s32[]{:S(2)}) async-start(s8[10616832]{0:T(1024)(128)(4,1)} %bitcast.9), calls=%async_computation.4 | async-start | bytes 4456448
  178.3 10.2 %slice-start.1 = ((s8[10616832]{0:T(1024)(128)(4,1)}), s8[4194304]{0:T(1024)(128)(4,1)S(1)}, s32[]{:S(2)}) async-start(s8[10616832]{0:T(1024)(128)(4,1)} %bitcast.9), calls=%async_computation.5 | async-start | bytes 8388608
  178.3 10.2 %slice-start.2 = ((s8[10616832]{0:T(1024)(128)(4,1)}), s8[4194304]{0:T(1024)(128)(4,1)S(1)}, s32[]{:S(2)}) async-start(s8[10616832]{0:T(1024)(128)(4,1)} %bitcast.9), calls=%async_computation.6 | async-start | bytes 8388608
  188.4 7.3 %copy-start = (f32[2304,1152]{1,0:T(8,128)}, f32[2304,1152]{1,0:T(8,128)S(1)}, u32[]{:S(2)}) copy-start(f32[2304,1152]{1,0:T(8,128)S(1)} %get-tuple-element.13) | copy-start | bytes 31850500
Sparse Core Ops, SparseCore 0:
  10.2 24.5 reduce-scatter.4
  37.1 123.6 reduce-scatter.2
where the time goes:
time: 203 us
  waiting for transfers between devices  125 us (62%)
  blocking collectives  33.6 us (17%)
  other arithmetic  28.1 us (14%)
  between operations  14.8 us (7%)
    reduce_scatter x1, waiting for transfers between devices, shards(): lax.psum_scatter(grad_down[0], 'dp', scatter_dimension=0, tiled=True)  98 us
    reduce_scatter x1, waiting for transfers between devices, shards(): lax.psum_scatter(grad_query[0], 'dp', scatter_dimension=0, tiled=True)  25.4 us
    psum x1, blocking collectives, shards(): head_total = lax.psum(head_part, ('dp', 'ctx'))  20.8 us
    psum x1, blocking collectives, shards(): neuron_total = lax.psum(neuron_part, ('dp', 'tensor'))  12.8 us
    convert_element_type x2, other arithmetic, finish(): return (parameter_new, moment_new, update.astype(jnp.bfloat16))  12.3 us
    sub x2, other arithmetic, finish(): parameter_new = parameter - LEARN_RATE * (update + DECAY_RATE * parameter)  9.24 us
    reduce_sum x1, other arithmetic, shards(): neuron_part = jnp.sum(down_grad * down_grad, axis=0)  4.08 us
  transfers between devices with their start and end apart: 2, of which 2 were waited for; matrix products, arithmetic and copies ran while one was open for 4% of the time, Pallas kernels for 0%

commit v1 on v0

v1 whole, which is shorter than its diff:
```python
import functools

import jax
import jax.numpy as jnp
from jax import lax
from jax.experimental import pallas as pl
from jax.experimental.pallas import tpu as pltpu
from jax.sharding import PartitionSpec as P

HEAD_DIM = 128
LANES = 128

BETA_ONE = 0.9
BETA_TWO = 0.95
EPSILON = 1e-08
LEARN_RATE = 0.003
DECAY_RATE = 0.1

ANY = pl.BlockSpec(memory_space=pl.ANY)


def tile_of(rows, most):
    tile = min(rows, most) // 16 * 16
    while tile > 16 and rows % tile:
        tile -= 16
    return tile if tile and rows % tile == 0 else rows


def pad(width):
    return -(-width // LANES) * LANES


def cost(byte_count, flops=0):
    return pl.CostEstimate(flops=flops, bytes_accessed=byte_count, transcendentals=0)


def cut(gradient, part, first, blocks, rows, after):
    tile = tile_of(rows, 768)
    steps = rows // tile

    def kernel(part_ref, grad_ref, *rest):
        rest[-1][...] = grad_ref[0]

    return pl.pallas_call(
        kernel,
        grid_spec=pltpu.PrefetchScalarGridSpec(
            num_scalar_prefetch=1,
            grid=(blocks, steps),
            in_specs=[pl.BlockSpec((1, tile, LANES), lambda c, i, p: (0, p[0] * steps + i, first + c))]
            + [ANY] * len(after),
            out_specs=pl.BlockSpec((tile, LANES), lambda c, i, p: (i, c)),
        ),
        out_shape=jax.ShapeDtypeStruct((rows, blocks * LANES), gradient.dtype),
        cost_estimate=cost(4 * rows * blocks * LANES),
        name="cut",
    )(part[None], gradient, *after)


def gather_moment(gradient, received, moment, moment_new, me, first, blocks, replicas):
    rows = moment.shape[0]
    tile = tile_of(rows, 768)
    steps = rows // tile
    count = len(received)

    def kernel(me_ref, grad_ref, *rest):
        received_refs, moment_ref = rest[:count], rest[count]
        moment_out, sum_out = rest[-2:]
        total = grad_ref[0].astype(jnp.float32)
        for ref in received_refs:
            total = total + ref[...].astype(jnp.float32)
        mean = total * (1.0 / replicas) if replicas & (replicas - 1) == 0 else total / replicas
        moment_out[...] = BETA_ONE * moment_ref[...] + (1.0 - BETA_ONE) * mean
        squares = jnp.sum(mean * mean, axis=0, keepdims=True)

        @pl.when(pl.program_id(1) == 0)
        def _():
            sum_out[...] = squares

        @pl.when(pl.program_id(1) != 0)
        def _():
            sum_out[...] += squares

    chained = [] if moment_new is None else [moment_new]
    return pl.pallas_call(
        kernel,
        grid_spec=pltpu.PrefetchScalarGridSpec(
            num_scalar_prefetch=1,
            grid=(blocks, steps),
            in_specs=[pl.BlockSpec((1, tile, LANES), lambda c, i, p: (0, p[0] * steps + i, first + c))]
            + [pl.BlockSpec((tile, LANES), lambda c, i, p: (i, c))] * count
            + [pl.BlockSpec((tile, LANES), lambda c, i, p: (i, first + c))]
            + [ANY] * len(chained),
            out_specs=[
                pl.BlockSpec((tile, LANES), lambda c, i, p: (i, first + c)),
                pl.BlockSpec((1, LANES), lambda c, i, p: (0, c)),
            ],
        ),
        out_shape=[
            jax.ShapeDtypeStruct(moment.shape, jnp.float32),
            jax.ShapeDtypeStruct((1, blocks * LANES), jnp.float32),
        ],
        input_output_aliases={3 + count: 0} if chained else {},
        cost_estimate=cost((10 + 2 * count) * rows * blocks * LANES),
        name="gather_moment",
    )(me[None], gradient, *received, moment, *chained)


def finish(keep, second_wide, parameter, moment_new, chained, first, blocks):
    rows = parameter.shape[0]
    tile = tile_of(rows, 768)

    def kernel(keep_ref, second_ref, parameter_ref, moment_ref, *rest):
        parameter_out, update_out = rest[-2:]
        below = jnp.sqrt(second_ref[...] / keep_ref[1]) + EPSILON
        scale = 1.0 / (keep_ref[0] * below)
        update = moment_ref[...] * scale
        value = parameter_ref[...]
        parameter_out[...] = value - LEARN_RATE * (update + DECAY_RATE * value)
        update_out[...] = update.astype(jnp.bfloat16)

    wide = pl.BlockSpec((tile, LANES), lambda c, i: (i, first + c))
    aliases = {3: 0}
    if chained:
        aliases.update({4: 1, 5: 2})
    return pl.pallas_call(
        kernel,
        grid=(blocks, rows // tile),
        in_specs=[
            pl.BlockSpec(memory_space=pltpu.SMEM),
            pl.BlockSpec((1, LANES), lambda c, i: (0, c)),
            wide,
            wide,
        ]
        + [ANY] * len(chained),
        out_specs=[ANY, wide, wide],
        out_shape=[
            jax.ShapeDtypeStruct(parameter.shape, jnp.float32),
            jax.ShapeDtypeStruct(parameter.shape, jnp.float32),
            jax.ShapeDtypeStruct(parameter.shape, jnp.bfloat16),
        ],
        input_output_aliases=aliases,
        cost_estimate=cost(14 * rows * blocks * LANES),
        name="finish",
    )(keep, second_wide, parameter, moment_new, *chained)


def total_over(value, axes):
    size = 1
    for axis in axes:
        size *= lax.axis_size(axis)
    if size > 8 or size & (size - 1):
        return lax.psum(value, axes)
    terms = [value] + [
        lax.ppermute(value, axes, [(i, i ^ k) for i in range(size)]) for k in range(1, size)
    ]
    while len(terms) > 1:
        terms = [a + b for a, b in zip(terms[::2], terms[1::2])]
    return terms[0]


def exchange(gradient, rows, first, blocks, me, after):
    replicas = lax.axis_size("dp")
    received = []
    for d in range(1, replicas):
        part = lax.rem(me + d, replicas)
        piece = cut(gradient, part, first, blocks, rows, after)
        received.append(lax.ppermute(piece, "dp", [(i, (i + d) % replicas) for i in range(replicas)]))
    return received


def plan(blocks):
    sizes, left = [], blocks
    while left > 3:
        sizes.append(min(2, left - 3))
        left -= sizes[-1]
    early = len(sizes)
    return sizes + [1] * left, early


def shards(
    grad_down,
    grad_query,
    down_param,
    down_moment,
    down_second,
    query_param,
    query_moment,
    query_second,
    step_count,
):
    replicas = lax.axis_size("dp")
    me = lax.axis_index("dp").astype(jnp.int32)
    step_value = step_count[0].astype(jnp.float32)
    keep = jnp.stack(
        [
            1.0 - jnp.power(jnp.float32(BETA_ONE), step_value),
            1.0 - jnp.power(jnp.float32(BETA_TWO), step_value),
        ]
    )
    down_rows, down_cols = down_param.shape
    query_rows, query_cols = query_param.shape
    neuron_count = grad_down.shape[1] * lax.axis_size("tensor")
    head_count = grad_query.shape[1] * lax.axis_size("ctx") * HEAD_DIM
    query_blocks = query_cols // LANES

    sizes, early = plan(pad(down_cols) // LANES)
    starts = [sum(sizes[:k]) for k in range(len(sizes))]

    query_received = exchange(grad_query, query_rows, 0, query_blocks, me, [])
    down_received = [exchange(grad_down, down_rows, starts[k], sizes[k], me, []) for k in range(min(2, len(sizes)))]

    query_moment_new, query_sum = gather_moment(
        grad_query, query_received, query_moment, None, me, 0, query_blocks, replicas
    )
    done = [query_sum]
    down_moment_new = None
    down_sums = []
    groups = [(0, early), (early, len(sizes) - 1), (len(sizes) - 1, len(sizes))]
    groups = [g for g in groups if g[0] < g[1]]
    seconds = []
    chained = []
    pending = None
    for k in range(len(sizes)):
        if k + 2 < len(sizes):
            down_received.append(exchange(grad_down, down_rows, starts[k + 2], sizes[k + 2], me, done))
        down_moment_new, squares = gather_moment(
            grad_down, down_received[k], down_moment, down_moment_new, me, starts[k], sizes[k], replicas
        )
        down_sums.append(squares)
        done = [squares]
        for low, high in groups:
            if high != k + 1:
                continue
            begin = starts[low] * LANES
            end = min(begin + sum(sizes[low:high]) * LANES, down_cols)
            part = jnp.concatenate(down_sums[low:high], axis=1)
            total = total_over(part, ("dp", "tensor"))
            old = jnp.pad(down_second[begin:end], (0, part.shape[1] - (end - begin)))[None]
            second = BETA_TWO * old + (1.0 - BETA_TWO) * (total / neuron_count)
            seconds.append(second[0, : end - begin])
            if pending is not None:
                down_moment_new, *chained = finish(
                    keep, pending[0], down_param, down_moment_new, chained, pending[1], pending[2]
                )
            pending = (second, starts[low], sum(sizes[low:high]))
            if low == 0:
                head_part = jnp.sum(query_sum.reshape(query_blocks, HEAD_DIM), axis=1)[None]
                head_total = total_over(head_part, ("dp", "ctx"))[0]
                query_second_new = BETA_TWO * query_second + (1.0 - BETA_TWO) * (head_total / head_count)
                query_moment_new, query_param_new, query_update = finish(
                    keep,
                    jnp.repeat(query_second_new, HEAD_DIM)[None],
                    query_param,
                    query_moment_new,
                    [],
                    0,
                    query_blocks,
                )
    down_moment_new, *chained = finish(
        keep, pending[0], down_param, down_moment_new, chained, pending[1], pending[2]
    )
    down_param_new, down_update = chained
    return (
        down_param_new,
        down_moment_new,
        jnp.concatenate(seconds),
        down_update,
        query_param_new,
        query_moment_new,
        query_second_new,
        query_update,
    )


def solution(mesh):
    in_specs = (
        P("dp", "tensor", "ctx"),
        P("dp", "ctx", "tensor"),
        P(("tensor", "dp"), "ctx"),
        P(("tensor", "dp"), "ctx"),
        P("ctx"),
        P(("ctx", "dp"), "tensor"),
        P(("ctx", "dp"), "tensor"),
        P("tensor"),
        P(),
    )
    out_specs = (
        P(("tensor", "dp"), "ctx"),
        P(("tensor", "dp"), "ctx"),
        P("ctx"),
        P(("tensor", "dp"), "ctx"),
        P(("ctx", "dp"), "tensor"),
        P(("ctx", "dp"), "tensor"),
        P("tensor"),
        P(("ctx", "dp"), "tensor"),
    )
    return jax.shard_map(shards, mesh=mesh, in_specs=in_specs, out_specs=out_specs, check_vma=False)
```

time: 203 us -> 193 us (0.951)
  Pallas kernels: 0 us -> 85.5 us
  waiting for transfers between devices: 125 us -> 49.3 us
  starting transfers between devices: 0.08 us -> 47.2 us
  blocking collectives: 33.6 us -> 0 us
  other arithmetic: 28.1 us -> 3.11 us
  between operations: 14.8 us -> 1.56 us
  local copies, waits for them, and re-layouts: 1.16 us -> 4.87 us
    reduce_scatter x2 -> x0, waiting for transfers between devices: 123 us -> none  [the longest x1 98 us: shards(): lax.psum_scatter(grad_down[0], 'dp', scatter_dimension=0, tiled=True)]
    pallas_call x0 -> x18, Pallas kernels: none -> 85.5 us  [the longest x7 32.1 us: gather_moment(): pl.pallas_call(kernel, grid_spec=pltpu.PrefetchScalarGridSpec(num_scalar_...]
    ppermute x0 -> x35, waiting for transfers between devices: none -> 49.3 us  [the longest x7 25.2 us: exchange(): lax.ppermute(piece, 'dp', [(i, (i + d) % replicas) for i in range(replica...]
    ppermute x0 -> x35, starting transfers between devices: none -> 47.2 us  [the longest x28 35.1 us: total_over(): lax.ppermute(value, axes, [(i, i ^ k) for i in range(size)])]
    psum x2 -> x0, blocking collectives: 33.6 us -> none  [the longest x1 20.8 us: shards(): head_total = lax.psum(head_part, ('dp', 'ctx'))]
    convert_element_type x2 -> x0, other arithmetic: 12.3 us -> none  [finish(): return (parameter_new, moment_new, update.astype(jnp.bfloat16))]
    sub x2 -> x0, other arithmetic: 9.24 us -> none  [finish(): parameter_new = parameter - LEARN_RATE * (update + DECAY_RATE * parameter)]
    reduce_sum x3 -> x1, other arithmetic: 5.46 us -> 0.12 us  [shards(): head_part = jnp.sum(query_sum.reshape(query_blocks, HEAD_DIM), axis=1)[None]]
  transfers between devices with their start and end apart: 2 -> 35, of which waited for: 2 -> 5; matrix products, arithmetic and copies ran while one was open for 4% -> 2% of each run, Pallas kernels for 0% -> 41%
where the time goes in v1:
time: 193 us; the launch traced here: 192 us
  Pallas kernels  85.5 us (44%)
  waiting for transfers between devices  49.3 us (26%)
  starting transfers between devices  47.2 us (24%)
  local copies, waits for them, and re-layouts  4.87 us (3%)
  other arithmetic  3.11 us (2%)
    ppermute x28, starting transfers between devices, total_over(): lax.ppermute(value, axes, [(i, i ^ k) for i in range(size)])  35.1 us
    pallas_call x7, Pallas kernels, gather_moment(): pl.pallas_call(kernel, grid_spec=pltpu.PrefetchScalarGridSpec(num_scalar_...  32.1 us
    pallas_call x4, Pallas kernels, finish(): pl.pallas_call(kernel, grid=(blocks, rows // tile), in_specs=[pl.BlockSpe...  28.8 us
    ppermute x7, waiting for transfers between devices, exchange(): lax.ppermute(piece, 'dp', [(i, (i + d) % replicas) for i in range(replica...  25.2 us
    pallas_call x7, Pallas kernels, cut(): pl.pallas_call(kernel, grid_spec=pltpu.PrefetchScalarGridSpec(num_scalar_...  24.6 us
    ppermute x28, waiting for transfers between devices, total_over(): lax.ppermute(value, axes, [(i, i ^ k) for i in range(size)])  24.1 us
    ppermute x7, starting transfers between devices, exchange(): lax.ppermute(piece, 'dp', [(i, (i + d) % replicas) for i in range(replica...  12.2 us
  transfers between devices with their start and end apart: 35, of which 5 were waited for; matrix products, arithmetic and copies ran while one was open for 2% of the time, Pallas kernels for 41%

profile of v1, /device:TPU:0, one launch (start us, length us, event | category | flops | bytes accessed | tf_op | source)
XLA Modules:
  0.0 191.5 jit_solution(5047166871863641890)
XLA Ops:
  0.6 3.2 %cut.7 = bf16[576,512]{1,0:T(8,128)(2,1)} custom-call(s32[1]{0:T(128)} %bitcast.2.part_ref, bf16[1,1152,512]{2,1,0:T(8,128)(2,1)} %grad_ref.15), custom_call_target="tpu_custom_call" | custom-call | bytes 1179648 | tf_op jit(solution)/shard_map/cut/pallas_call | solution.py:44
  3.8 3.0 %collective-permute-start = (bf16[576,512]{1,0:T(8,128)(2,1)}, bf16[576,512]{1,0:T(8,128)(2,1)S(1)}, u32[]{:S(2)}, u32[]{:S(2)}) collective-permute-start(bf16[576,512]{1,0:T(8,128)(2,1)} %cut.7), channel_id=1, source_target_pairs={{0,16},{16,0},{1,17},{17,1},{2,18},{18,2},{3,19},{19,3},{4,20},{20... | collective-permute-start | bytes 1769480 | tf_op jit(solution)/shard_map/ppermute | solution.py:167
  6.8 4.4 %cut.10 = bf16[2304,256]{1,0:T(8,128)(2,1)} custom-call(s32[1]{0:T(128)} %bitcast.2.part_ref, bf16[1,4608,1152]{2,1,0:T(8,128)(2,1)} %grad_ref.27), custom_call_target="tpu_custom_call" | custom-call | bytes 2359296 | tf_op jit(solution)/shard_map/cut/pallas_call | solution.py:44
  11.2 4.4 %cut.9 = bf16[2304,256]{1,0:T(8,128)(2,1)} custom-call(s32[1]{0:T(128)} %bitcast.2.part_ref, bf16[1,4608,1152]{2,1,0:T(8,128)(2,1)} %grad_ref.27), custom_call_target="tpu_custom_call" | custom-call | bytes 2359296 | tf_op jit(solution)/shard_map/cut/pallas_call | solution.py:44
  17.6 3.6 %collective-permute-done.rest_0_ = bf16[576,512]{1,0:T(8,128)(2,1)S(1)} collective-permute-done((bf16[576,512]{1,0:T(8,128)(2,1)}, bf16[576,512]{1,0:T(8,128)(2,1)S(1)}, u32[]{:S(2)}, u32[]{:S(2)}) %collective-permute-start) | collective-permute-done | bytes 589856 | tf_op jit(solution)/shard_map/ppermute | solution.py:167
  22.0 3.8 %gather_moment.7 = (f32[576,512]{1,0:T(8,128)}, f32[1,512]{1,0:T(1,128)}) custom-call(s32[1]{0:T(128)} %bitcast.1.me_ref, bf16[1,1152,512]{2,1,0:T(8,128)(2,1)} %grad_ref.15, bf16[576,512]{1,0:T(8,128)(2,1)} %copy-done.3, f32[576,512]{1,0:T(8,128)} %rest_1_.7), custom_call_target="tpu_custom_call" | custom-call | bytes 3538944 | tf_op jit(solution)/shard_map/gather_moment/pallas_call | solution.py:84
  25.9 4.4 %cut.8 = bf16[2304,256]{1,0:T(8,128)(2,1)} custom-call(s32[1]{0:T(128)} %bitcast.2.part_ref, bf16[1,4608,1152]{2,1,0:T(8,128)(2,1)} %grad_ref.27, f32[1,512]{1,0:T(1,128)} %get-tuple-element.34.rest_0_), custom_call_target="tpu_custom_call" | custom-call | bytes 2359296 | tf_op jit(solution)/shard_map/cut/pallas_call | solution.py:44
  33.0 13.5 %collective-permute-done.3.rest_0_ = bf16[2304,256]{1,0:T(8,128)(2,1)S(1)} collective-permute-done((bf16[2304,256]{1,0:T(8,128)(2,1)}, bf16[2304,256]{1,0:T(8,128)(2,1)S(1)}, u32[]{:S(2)}, u32[]{:S(2)}) %collective-permute-start.3) | collective-permute-done | bytes 1179680 | tf_op jit(solution)/shard_map/ppermute | solution.py:167
  47.5 5.7 %gather_moment.8 = (f32[2304,1152]{1,0:T(8,128)}, f32[1,256]{1,0:T(1,128)}) custom-call(s32[1]{0:T(128)} %bitcast.1.me_ref, bf16[1,4608,1152]{2,1,0:T(8,128)(2,1)} %grad_ref.27, bf16[2304,256]{1,0:T(8,128)(2,1)} %copy-done.2, f32[2304,1152]{1,0:T(8,128)} %rest_1_.13), custom_call_target="tpu_custom_call" | custom-call | bytes 7077888 | tf_op jit(solution)/shard_map/gather_moment/pallas_call | solution.py:84
  53.2 2.7 %cut.13 = bf16[2304,128]{1,0:T(8,128)(2,1)} custom-call(s32[1]{0:T(128)} %bitcast.2.part_ref, bf16[1,4608,1152]{2,1,0:T(8,128)(2,1)} %grad_ref.27, f32[1,256]{1,0:T(1,128)} %get-tuple-element.38.rest_0_), custom_call_target="tpu_custom_call" | custom-call | bytes 1179648 | tf_op jit(solution)/shard_map/cut/pallas_call | solution.py:44
  63.7 8.1 %collective-permute-done.2.rest_0_ = bf16[2304,256]{1,0:T(8,128)(2,1)S(1)} collective-permute-done((bf16[2304,256]{1,0:T(8,128)(2,1)}, bf16[2304,256]{1,0:T(8,128)(2,1)S(1)}, u32[]{:S(2)}, u32[]{:S(2)}) %collective-permute-start.2) | collective-permute-done | bytes 1179680 | tf_op jit(solution)/shard_map/ppermute | solution.py:167
  73.8 5.7 %gather_moment.9 = (f32[2304,1152]{1,0:T(8,128)}, f32[1,256]{1,0:T(1,128)}) custom-call(s32[1]{0:T(128)} %bitcast.1.me_ref, bf16[1,4608,1152]{2,1,0:T(8,128)(2,1)} %grad_ref.27, bf16[2304,256]{1,0:T(8,128)(2,1)} %copy-done.1, f32[2304,1152]{1,0:T(8,128)} %rest_1_.13, f32[2304,1152]{1,0:T(8,128)} %get-tuple-element.35.rest_2_), custom_call_target="tpu_custom_call", output_to_operand_aliasing={{0}: (4, {})} | custom-call | bytes 7077888 | tf_op jit(solution)/shard_map/gather_moment/pallas_call | solution.py:84
  79.6 2.8 %cut.12 = bf16[2304,128]{1,0:T(8,128)(2,1)} custom-call(s32[1]{0:T(128)} %bitcast.2.part_ref, bf16[1,4608,1152]{2,1,0:T(8,128)(2,1)} %grad_ref.27, f32[1,256]{1,0:T(1,128)} %get-tuple-element.39.rest_0_), custom_call_target="tpu_custom_call" | custom-call | bytes 1179648 | tf_op jit(solution)/shard_map/cut/pallas_call | solution.py:44
  86.9 22.0 %collective-permute-done.31 = f32[1,4]{1,0:T(1,128)S(1)} collective-permute-done((f32[1,4]{1,0:T(1,128)S(1)}, f32[1,4]{1,0:T(1,128)S(1)}, u32[]{:S(2)}, u32[]{:S(2)}) %collective-permute-start.31) | collective-permute-done | bytes 48 | tf_op jit(solution)/shard_map/ppermute | solution.py:154
  109.0 3.8 %collective-permute-start.30 = (f32[1,4]{1,0:T(1,128)S(1)}, f32[1,4]{1,0:T(1,128)S(1)}, u32[]{:S(2)}, u32[]{:S(2)}) collective-permute-start(f32[1,4]{1,0:T(1,128)S(1)} %bitcast.23), channel_id=1, source_target_pairs={{0,3},{1,2},{2,1},{3,0},{16,19},{17,18},{18,17},{19,16},{4,7},{5,6... | collective-permute-start | bytes 56 | tf_op jit(solution)/shard_map/ppermute | solution.py:154
  117.4 5.7 %gather_moment.10 = (f32[2304,1152]{1,0:T(8,128)}, f32[1,256]{1,0:T(1,128)}) custom-call(s32[1]{0:T(128)} %bitcast.1.me_ref, bf16[1,4608,1152]{2,1,0:T(8,128)(2,1)} %grad_ref.27, bf16[2304,256]{1,0:T(8,128)(2,1)} %copy-done, f32[2304,1152]{1,0:T(8,128)} %rest_1_.13, f32[2304,1152]{1,0:T(8,128)} %get-tuple-element.36.rest_2_), custom_call_target="tpu_custom_call", output_to_operand_aliasing={{0}: (4, {})} | custom-call | bytes 7077888 | tf_op jit(solution)/shard_map/gather_moment/pallas_call | solution.py:84
  123.2 2.8 %cut.11 = bf16[2304,128]{1,0:T(8,128)(2,1)} custom-call(s32[1]{0:T(128)} %bitcast.2.part_ref, bf16[1,4608,1152]{2,1,0:T(8,128)(2,1)} %grad_ref.27, f32[1,256]{1,0:T(1,128)} %get-tuple-element.37.rest_0_), custom_call_target="tpu_custom_call" | custom-call | bytes 1179648 | tf_op jit(solution)/shard_map/cut/pallas_call | solution.py:44
  130.6 3.7 %gather_moment.11 = (f32[2304,1152]{1,0:T(8,128)}, f32[1,128]{1,0:T(1,128)}) custom-call(s32[1]{0:T(128)} %bitcast.1.me_ref, bf16[1,4608,1152]{2,1,0:T(8,128)(2,1)} %grad_ref.27, bf16[2304,128]{1,0:T(8,128)(2,1)} %copy-done.5, f32[2304,1152]{1,0:T(8,128)} %rest_1_.13, f32[2304,1152]{1,0:T(8,128)} %get-tuple-element.40.rest_2_), custom_call_target="tpu_custom_call", output_to_operand_aliasing={{0}: (4, {})} | custom-call | bytes 3538944 | tf_op jit(solution)/shard_map/gather_moment/pallas_call | solution.py:84
  136.3 3.7 %gather_moment.12 = (f32[2304,1152]{1,0:T(8,128)}, f32[1,128]{1,0:T(1,128)}) custom-call(s32[1]{0:T(128)} %bitcast.1.me_ref, bf16[1,4608,1152]{2,1,0:T(8,128)(2,1)} %grad_ref.27, bf16[2304,128]{1,0:T(8,128)(2,1)} %copy-done.6, f32[2304,1152]{1,0:T(8,128)} %rest_1_.13, f32[2304,1152]{1,0:T(8,128)} %get-tuple-element.41.rest_2_), custom_call_target="tpu_custom_call", output_to_operand_aliasing={{0}: (4, {})} | custom-call | bytes 3538944 | tf_op jit(solution)/shard_map/gather_moment/pallas_call | solution.py:84
  150.0 15.3 %finish.4 = (f32[2304,1152]{1,0:T(8,128)}, f32[2304,1152]{1,0:T(8,128)}, bf16[2304,1152]{1,0:T(8,128)(2,1)}) custom-call(f32[2]{0:T(128)} %pad_maximum_fusion.1.keep_ref, f32[1,768]{1,0:T(1,128)} %get-tuple-element.61.second_ref, f32[2304,1152]{1,0:T(8,128)} %parameter_ref.6, f32[2304,1152]{1,0:T(8,128)} %get-tuple-element.42.moment_ref), custom_call_target="tpu_custom_call", output_to_operand_aliasing={{0}: (3, {})} | custom-call | bytes 24772608 | tf_op jit(solution)/shard_map/finish/pallas_call | solution.py:125
  165.3 3.7 %gather_moment.13 = (f32[2304,1152]{1,0:T(8,128)}, f32[1,128]{1,0:T(1,128)}) custom-call(s32[1]{0:T(128)} %bitcast.1.me_ref, bf16[1,4608,1152]{2,1,0:T(8,128)(2,1)} %grad_ref.27, bf16[2304,128]{1,0:T(8,128)(2,1)} %copy-done.4, f32[2304,1152]{1,0:T(8,128)} %rest_1_.13, f32[2304,1152]{1,0:T(8,128)} %get-tuple-element.43.rest_2_), custom_call_target="tpu_custom_call", output_to_operand_aliasing={{0}: (4, {})} | custom-call | bytes 3538944 | tf_op jit(solution)/shard_map/gather_moment/pallas_call | solution.py:84
  172.1 3.9 %finish.7 = (f32[576,512]{1,0:T(8,128)}, f32[576,512]{1,0:T(8,128)}, bf16[576,512]{1,0:T(8,128)(2,1)}) custom-call(f32[2]{0:T(128)} %pad_maximum_fusion.1.keep_ref, f32[1,512]{1,0:T(1,128)} %bitcast.15, f32[576,512]{1,0:T(8,128)} %parameter_ref.7, f32[576,512]{1,0:T(8,128)} %get-tuple-element.56.moment_ref), custom_call_target="tpu_custom_call", output_to_operand_aliasing={{0}: (3, {})} | custom-call | bytes 4128768 | tf_op jit(solution)/shard_map/finish/pallas_call | solution.py:125
  180.7 5.8 %finish.5 = (f32[2304,1152]{1,0:T(8,128)}, f32[2304,1152]{1,0:T(8,128)}, bf16[2304,1152]{1,0:T(8,128)(2,1)}) custom-call(f32[2]{0:T(128)} %pad_maximum_fusion.1.keep_ref, f32[1,256]{1,0:T(1,128)} %multiply_add_fusion.1.second_ref, f32[2304,1152]{1,0:T(8,128)} %parameter_ref.6, ...), custom_call_target="tpu_custom_call", output_to_operand_aliasing={{0}: (3, {}), {1}: (4, {}), {2}: (5, {})} | custom-call | bytes 8257536 | tf_op jit(solution)/shard_map/finish/pallas_call | solution.py:125
  187.1 3.7 %finish.6 = (f32[2304,1152]{1,0:T(8,128)}, f32[2304,1152]{1,0:T(8,128)}, bf16[2304,1152]{1,0:T(8,128)(2,1)}) custom-call(f32[2]{0:T(128)} %pad_maximum_fusion.1.keep_ref, f32[1,128]{1,0:T(1,128)} %bitcast_add_fusion.1.second_ref, f32[2304,1152]{1,0:T(8,128)} %parameter_ref.6, ...), custom_call_target="tpu_custom_call", output_to_operand_aliasing={{0}: (3, {}), {1}: (4, {}), {2}: (5, {})} | custom-call | bytes 4128768 | tf_op jit(solution)/shard_map/finish/pallas_call | solution.py:125
  (113 shorter events, 50.4 us)
Async XLA Ops:
  3.8 17.4 %collective-permute-start = (bf16[576,512]{1,0:T(8,128)(2,1)}, bf16[576,512]{1,0:T(8,128)(2,1)S(1)}, u32[]{:S(2)}, u32[]{:S(2)}) collective-permute-start(bf16[576,512]{1,0:T(8,128)(2,1)} %cut.7), channel_id=1, source_target_pairs={{0,16},{16,0},{1,17},{17,1},{2,18},{18,2},{3,19},{19,3},{4,20},{20... | collective-permute-start | bytes 1769480 | tf_op jit(solution)/shard_map/ppermute | solution.py:167
  11.2 35.3 %collective-permute-start.3 = (bf16[2304,256]{1,0:T(8,128)(2,1)}, bf16[2304,256]{1,0:T(8,128)(2,1)S(1)}, u32[]{:S(2)}, u32[]{:S(2)}) collective-permute-start(bf16[2304,256]{1,0:T(8,128)(2,1)} %cut.10), channel_id=1, source_target_pairs={{0,16},{16,0},{1,17},{17,1},{2,18},{18,2},{3,19},{19,3},{4,20},{20... | collective-permute-start | bytes 3538952 | tf_op jit(solution)/shard_map/ppermute | solution.py:167
  15.6 56.2 %collective-permute-start.2 = (bf16[2304,256]{1,0:T(8,128)(2,1)}, bf16[2304,256]{1,0:T(8,128)(2,1)S(1)}, u32[]{:S(2)}, u32[]{:S(2)}) collective-permute-start(bf16[2304,256]{1,0:T(8,128)(2,1)} %cut.9), channel_id=1, source_target_pairs={{0,16},{16,0},{1,17},{17,1},{2,18},{18,2},{3,19},{19,3},{4,20},{20... | collective-permute-start | bytes 3538952 | tf_op jit(solution)/shard_map/ppermute | solution.py:167
  30.2 86.2 %collective-permute-start.1 = (bf16[2304,256]{1,0:T(8,128)(2,1)}, bf16[2304,256]{1,0:T(8,128)(2,1)S(1)}, u32[]{:S(2)}, u32[]{:S(2)}) collective-permute-start(bf16[2304,256]{1,0:T(8,128)(2,1)} %cut.8), channel_id=1, source_target_pairs={{0,16},{16,0},{1,17},{17,1},{2,18},{18,2},{3,19},{19,3},{4,20},{20... | collective-permute-start | bytes 3538952 | tf_op jit(solution)/shard_map/ppermute | solution.py:167
  56.0 73.0 %collective-permute-start.13 = (bf16[2304,128]{1,0:T(8,128)(2,1)}, bf16[2304,128]{1,0:T(8,128)(2,1)S(1)}, u32[]{:S(2)}, u32[]{:S(2)}) collective-permute-start(bf16[2304,128]{1,0:T(8,128)(2,1)} %cut.13), channel_id=1, source_target_pairs={{0,16},{16,0},{1,17},{17,1},{2,18},{18,2},{3,19},{19,3},{4,20},{20... | collective-permute-start | bytes 1769480 | tf_op jit(solution)/shard_map/ppermute | solution.py:167
  58.8 23.5 %collective-permute-start.33 = (f32[1,4]{1,0:T(1,128)S(1)}, f32[1,4]{1,0:T(1,128)S(1)}, u32[]{:S(2)}, u32[]{:S(2)}) collective-permute-start(f32[1,4]{1,0:T(1,128)S(1)} %bitcast.18), channel_id=1, source_target_pairs={{0,18},{1,19},{2,16},{3,17},{16,2},{17,3},{18,0},{19,1},{4,22},{5,... | collective-permute-start | bytes 56 | tf_op jit(solution)/shard_map/ppermute | solution.py:154
  61.4 23.0 %collective-permute-start.34 = (f32[1,4]{1,0:T(1,128)S(1)}, f32[1,4]{1,0:T(1,128)S(1)}, u32[]{:S(2)}, u32[]{:S(2)}) collective-permute-start(f32[1,4]{1,0:T(1,128)S(1)} %bitcast.19), channel_id=1, source_target_pairs={{0,19},{1,18},{2,17},{3,16},{16,3},{17,2},{18,1},{19,0},{4,23},{5,... | collective-permute-start | bytes 56 | tf_op jit(solution)/shard_map/ppermute | solution.py:154
  71.8 37.2 %collective-permute-start.31 = (f32[1,4]{1,0:T(1,128)S(1)}, f32[1,4]{1,0:T(1,128)S(1)}, u32[]{:S(2)}, u32[]{:S(2)}) collective-permute-start(f32[1,4]{1,0:T(1,128)S(1)} %bitcast.20), channel_id=1, source_target_pairs={{0,16},{1,17},{2,18},{3,19},{16,0},{17,1},{18,2},{19,3},{4,20},{5,... | collective-permute-start | bytes 56 | tf_op jit(solution)/shard_map/ppermute | solution.py:154
  82.3 30.5 %collective-permute-start.32 = (f32[1,4]{1,0:T(1,128)S(1)}, f32[1,4]{1,0:T(1,128)S(1)}, u32[]{:S(2)}, u32[]{:S(2)}) collective-permute-start(f32[1,4]{1,0:T(1,128)S(1)} %bitcast.21), channel_id=1, source_target_pairs={{0,17},{1,16},{2,19},{3,18},{16,1},{17,0},{18,3},{19,2},{4,21},{5,... | collective-permute-start | bytes 56 | tf_op jit(solution)/shard_map/ppermute | solution.py:154
  84.4 28.4 %collective-permute-start.29 = (f32[1,4]{1,0:T(1,128)S(1)}, f32[1,4]{1,0:T(1,128)S(1)}, u32[]{:S(2)}, u32[]{:S(2)}) collective-permute-start(f32[1,4]{1,0:T(1,128)S(1)} %bitcast.22), channel_id=1, source_target_pairs={{0,2},{1,3},{2,0},{3,1},{16,18},{17,19},{18,16},{19,17},{4,6},{5,7... | collective-permute-start | bytes 56 | tf_op jit(solution)/shard_map/ppermute | solution.py:154
  112.8 22.1 %collective-permute-start.12 = (bf16[2304,128]{1,0:T(8,128)(2,1)}, bf16[2304,128]{1,0:T(8,128)(2,1)S(1)}, u32[]{:S(2)}, u32[]{:S(2)}) collective-permute-start(bf16[2304,128]{1,0:T(8,128)(2,1)} %cut.12), channel_id=1, source_target_pairs={{0,16},{16,0},{1,17},{17,1},{2,18},{18,2},{3,19},{19,3},{4,20},{20... | collective-permute-start | bytes 1769480 | tf_op jit(solution)/shard_map/ppermute | solution.py:167
  125.9 23.4 %collective-permute-start.4 = (bf16[2304,128]{1,0:T(8,128)(2,1)}, bf16[2304,128]{1,0:T(8,128)(2,1)S(1)}, u32[]{:S(2)}, u32[]{:S(2)}) collective-permute-start(bf16[2304,128]{1,0:T(8,128)(2,1)} %cut.11), channel_id=1, source_target_pairs={{0,16},{16,0},{1,17},{17,1},{2,18},{18,2},{3,19},{19,3},{4,20},{20... | collective-permute-start | bytes 1769480 | tf_op jit(solution)/shard_map/ppermute | solution.py:167
  127.5 12.5 %collective-permute-start.10 = (f32[1,768]{1,0:T(1,128)S(1)}, f32[1,768]{1,0:T(1,128)S(1)}, u32[]{:S(2)}, u32[]{:S(2)}) collective-permute-start(f32[1,768]{1,0:T(1,128)S(1)} %constant_dynamic-update-slice_fusion), channel_id=1, source_target_pairs={{0,24},{4,28},{8,16},{12,20},{16,8},{20,12},{24,0},{28,4},{1,25},{... | collective-permute-start | bytes 9224 | tf_op jit(solution)/shard_map/ppermute | solution.py:154
  129.0 12.5 %collective-permute-start.11 = (f32[1,768]{1,0:T(1,128)S(1)}, f32[1,768]{1,0:T(1,128)S(1)}, u32[]{:S(2)}, u32[]{:S(2)}) collective-permute-start(f32[1,768]{1,0:T(1,128)S(1)} %constant_dynamic-update-slice_fusion), channel_id=1, source_target_pairs={{0,28},{4,24},{8,20},{12,16},{16,12},{20,8},{24,4},{28,0},{1,29},{... | collective-permute-start | bytes 9224 | tf_op jit(solution)/shard_map/ppermute | solution.py:154
  129.0 12.6 %collective-permute-start.8 = (f32[1,768]{1,0:T(1,128)S(1)}, f32[1,768]{1,0:T(1,128)S(1)}, u32[]{:S(2)}, u32[]{:S(2)}) collective-permute-start(f32[1,768]{1,0:T(1,128)S(1)} %constant_dynamic-update-slice_fusion), channel_id=1, source_target_pairs={{0,16},{4,20},{8,24},{12,28},{16,0},{20,4},{24,8},{28,12},{1,17},{... | collective-permute-start | bytes 9224 | tf_op jit(solution)/shard_map/ppermute | solution.py:154
  145.1 23.9 %collective-permute-start.24 = (f32[1,256]{1,0:T(1,128)S(1)}, f32[1,256]{1,0:T(1,128)S(1)}, u32[]{:S(2)}, u32[]{:S(2)}) collective-permute-start(f32[1,256]{1,0:T(1,128)S(1)} %constant_dynamic-update-slice_fusion.3), channel_id=1, source_target_pairs={{0,16},{4,20},{8,24},{12,28},{16,0},{20,4},{24,8},{28,12},{1,17},{... | collective-permute-start | bytes 3080 | tf_op jit(solution)/shard_map/ppermute | solution.py:154
  146.2 24.8 %collective-permute-start.25 = (f32[1,256]{1,0:T(1,128)S(1)}, f32[1,256]{1,0:T(1,128)S(1)}, u32[]{:S(2)}, u32[]{:S(2)}) collective-permute-start(f32[1,256]{1,0:T(1,128)S(1)} %constant_dynamic-update-slice_fusion.3), channel_id=1, source_target_pairs={{0,20},{4,16},{8,28},{12,24},{16,4},{20,0},{24,12},{28,8},{1,21},{... | collective-permute-start | bytes 3080 | tf_op jit(solution)/shard_map/ppermute | solution.py:154
  147.8 28.2 %collective-permute-start.22 = (f32[1,256]{1,0:T(1,128)S(1)}, f32[1,256]{1,0:T(1,128)S(1)}, u32[]{:S(2)}, u32[]{:S(2)}) collective-permute-start(f32[1,256]{1,0:T(1,128)S(1)} %constant_dynamic-update-slice_fusion.3), channel_id=1, source_target_pairs={{0,8},{4,12},{8,0},{12,4},{16,24},{20,28},{24,16},{28,20},{1,9},{5... | collective-permute-start | bytes 3080 | tf_op jit(solution)/shard_map/ppermute | solution.py:154
  149.3 27.8 %collective-permute-start.23 = (f32[1,256]{1,0:T(1,128)S(1)}, f32[1,256]{1,0:T(1,128)S(1)}, u32[]{:S(2)}, u32[]{:S(2)}) collective-permute-start(f32[1,256]{1,0:T(1,128)S(1)} %constant_dynamic-update-slice_fusion.3), channel_id=1, source_target_pairs={{0,12},{4,8},{8,4},{12,0},{16,28},{20,24},{24,20},{28,16},{1,13},{... | collective-permute-start | bytes 3080 | tf_op jit(solution)/shard_map/ppermute | solution.py:154
  149.3 28.6 %collective-permute-start.21 = (f32[1,256]{1,0:T(1,128)S(1)}, f32[1,256]{1,0:T(1,128)S(1)}, u32[]{:S(2)}, u32[]{:S(2)}) collective-permute-start(f32[1,256]{1,0:T(1,128)S(1)} %constant_dynamic-update-slice_fusion.3), channel_id=1, source_target_pairs={{0,4},{4,0},{8,12},{12,8},{16,20},{20,16},{24,28},{28,24},{1,5},{5... | collective-permute-start | bytes 3080 | tf_op jit(solution)/shard_map/ppermute | solution.py:154
  169.0 10.5 %collective-permute-start.19 = (f32[1,128]{1,0:T(1,128)}, f32[1,128]{1,0:T(1,128)S(1)}, u32[]{:S(2)}, u32[]{:S(2)}) collective-permute-start(f32[1,128]{1,0:T(1,128)} %get-tuple-element.44), channel_id=1, source_target_pairs={{0,24},{4,28},{8,16},{12,20},{16,8},{20,12},{24,0},{28,4},{1,25},{... | collective-permute-start | bytes 1544 | tf_op jit(solution)/shard_map/ppermute | solution.py:154
  176.0 10.5 %collective-permute-start.17 = (f32[1,128]{1,0:T(1,128)}, f32[1,128]{1,0:T(1,128)S(1)}, u32[]{:S(2)}, u32[]{:S(2)}) collective-permute-start(f32[1,128]{1,0:T(1,128)} %get-tuple-element.44), channel_id=1, source_target_pairs={{0,16},{4,20},{8,24},{12,28},{16,0},{20,4},{24,8},{28,12},{1,17},{... | collective-permute-start | bytes 1544 | tf_op jit(solution)/shard_map/ppermute | solution.py:154
  177.1 9.4 %collective-permute-start.18 = (f32[1,128]{1,0:T(1,128)}, f32[1,128]{1,0:T(1,128)S(1)}, u32[]{:S(2)}, u32[]{:S(2)}) collective-permute-start(f32[1,128]{1,0:T(1,128)} %get-tuple-element.44), channel_id=1, source_target_pairs={{0,20},{4,16},{8,28},{12,24},{16,4},{20,0},{24,12},{28,8},{1,21},{... | collective-permute-start | bytes 1544 | tf_op jit(solution)/shard_map/ppermute | solution.py:154
  178.0 8.6 %collective-permute-start.15 = (f32[1,128]{1,0:T(1,128)}, f32[1,128]{1,0:T(1,128)S(1)}, u32[]{:S(2)}, u32[]{:S(2)}) collective-permute-start(f32[1,128]{1,0:T(1,128)} %get-tuple-element.44), channel_id=1, source_target_pairs={{0,8},{4,12},{8,0},{12,4},{16,24},{20,28},{24,16},{28,20},{1,9},{5... | collective-permute-start | bytes 1544 | tf_op jit(solution)/shard_map/ppermute | solution.py:154
  (28 other events, 263.6 us)

commit v2 on v1

--- a/solution.py
+++ b/solution.py
@@ -7,6 +7,7 @@
 from jax.experimental.pallas import tpu as pltpu
 from jax.sharding import PartitionSpec as P
 
+
 HEAD_DIM = 128
 LANES = 128
 
@@ -15,6 +16,7 @@
 EPSILON = 1e-08
 LEARN_RATE = 0.003
 DECAY_RATE = 0.1
+
 
 ANY = pl.BlockSpec(memory_space=pl.ANY)
 
@@ -66,8 +68,10 @@
         received_refs, moment_ref = rest[:count], rest[count]
         moment_out, sum_out = rest[-2:]
         total = grad_ref[0].astype(jnp.float32)
+        top = pl.multiple_of(pl.program_id(1) * tile, tile)
+        side = pl.multiple_of(pl.program_id(0) * LANES, LANES)
         for ref in received_refs:
-            total = total + ref[...].astype(jnp.float32)
+            total = total + ref[pl.ds(top, tile), pl.ds(side, LANES)].astype(jnp.float32)
         mean = total * (1.0 / replicas) if replicas & (replicas - 1) == 0 else total / replicas
         moment_out[...] = BETA_ONE * moment_ref[...] + (1.0 - BETA_ONE) * mean
         squares = jnp.sum(mean * mean, axis=0, keepdims=True)
@@ -87,7 +91,7 @@
             num_scalar_prefetch=1,
             grid=(blocks, steps),
             in_specs=[pl.BlockSpec((1, tile, LANES), lambda c, i, p: (0, p[0] * steps + i, first + c))]
-            + [pl.BlockSpec((tile, LANES), lambda c, i, p: (i, c))] * count
+            + [pl.BlockSpec(memory_space=pltpu.VMEM)] * count
             + [pl.BlockSpec((tile, LANES), lambda c, i, p: (i, first + c))]
             + [ANY] * len(chained),
             out_specs=[
@@ -158,12 +162,103 @@
     return terms[0]
 
 
-def exchange(gradient, rows, first, blocks, me, after):
+def peer_of(axes, sizes, step):
+    coordinates = {}
+    for axis, size in reversed(list(zip(axes, sizes))):
+        index, bits = lax.axis_index(axis), step % size
+        step //= size
+        bit = 1
+        while bit < size:
+            if bits & bit:
+                index = index + bit - 2 * bit * (index // bit % 2)
+            bit *= 2
+        coordinates[axis] = index
+    return coordinates
+
+
+def spread(values, axes_of, collective_id):
+    sizes_of = [tuple(lax.axis_size(axis) for axis in axes) for axes in axes_of]
+    counts = [functools.reduce(lambda a, b: a * b, sizes) for sizes in sizes_of]
+    number = len(values)
+
+    def kernel(*refs):
+        value_refs, out_refs = refs[:number], refs[number : 2 * number]
+        slot_refs = refs[2 * number : 3 * number]
+        send_refs, recv_refs = refs[3 * number : 4 * number], refs[4 * number :]
+        barrier = pltpu.get_barrier_semaphore()
+        for n in range(number):
+            for k in range(1, counts[n]):
+                pl.semaphore_signal(
+                    barrier,
+                    inc=1,
+                    device_id=peer_of(axes_of[n], sizes_of[n], k),
+                    device_id_type=pl.DeviceIdType.MESH,
+                )
+        pl.semaphore_wait(barrier, sum(counts) - number)
+        copies = []
+        for n in range(number):
+            for k in range(1, counts[n]):
+                copy = pltpu.make_async_remote_copy(
+                    src_ref=value_refs[n],
+                    dst_ref=slot_refs[n].at[k - 1],
+                    send_sem=send_refs[n].at[k - 1],
+                    recv_sem=recv_refs[n].at[k - 1],
+                    device_id=peer_of(axes_of[n], sizes_of[n], k),
+                    device_id_type=pl.DeviceIdType.MESH,
+                )
+                copy.start()
+                copies.append(copy)
+        for copy in copies:
+            copy.wait()
+        for n in range(number):
+            terms = [value_refs[n][...]] + [slot_refs[n][k - 1] for k in range(1, counts[n])]
+            while len(terms) > 1:
+                terms = [a + b for a, b in zip(terms[::2], terms[1::2])]
+            out_refs[n][...] = terms[0]
+
+    vmem = pl.BlockSpec(memory_space=pltpu.VMEM)
+    semaphores = [pltpu.SemaphoreType.DMA((max(count - 1, 1),)) for count in counts]
+    return pl.pallas_call(
+        kernel,
+        in_specs=[vmem] * number,
+        out_specs=[vmem] * number,
+        out_shape=[jax.ShapeDtypeStruct(value.shape, value.dtype) for value in values],
+        scratch_shapes=[
+            pltpu.VMEM((max(count - 1, 1),) + value.shape, value.dtype) for count, value in zip(counts, values)
+        ]
+        + semaphores
+        + semaphores,
+        compiler_params=pltpu.CompilerParams(collective_id=collective_id, has_side_effects=True),
+        cost_estimate=cost(8000000),
+        name="spread",
+    )(*values)
+
+
+def held(piece, after):
+    def kernel(*refs):
+        pass
+
+    return pl.pallas_call(
+        kernel,
+        in_specs=[ANY] * (1 + len(after)),
+        out_specs=ANY,
+        out_shape=jax.ShapeDtypeStruct(piece.shape, piece.dtype),
+        input_output_aliases={0: 0},
+        cost_estimate=cost(1000),
+        name="held",
+    )(piece, *after)
+
+
+def pieces_of(gradient, rows, first, blocks, me):
+    replicas = lax.axis_size("dp")
+    return [cut(gradient, lax.rem(me + d, replicas), first, blocks, rows, []) for d in range(1, replicas)]
+
+
+def send(pieces, after):
     replicas = lax.axis_size("dp")
     received = []
-    for d in range(1, replicas):
-        part = lax.rem(me + d, replicas)
-        piece = cut(gradient, part, first, blocks, rows, after)
+    for d, piece in enumerate(pieces, 1):
+        piece = held(piece, after) if after else piece
         received.append(lax.ppermute(piece, "dp", [(i, (i + d) % replicas) for i in range(replicas)]))
     return received
 
@@ -173,8 +268,11 @@
     while left > 3:
         sizes.append(min(2, left - 3))
         left -= sizes[-1]
-    early = len(sizes)
-    return sizes + [1] * left, early
+    early = max(len(sizes) - 1, 1)
+    middle = max(len(sizes), early)
+    sizes += [1] * left
+    groups = [(0, early), (early, middle), (middle, len(sizes))]
+    return sizes, [group for group in groups if group[0] < group[1]]
 
 
 def shards(
@@ -203,49 +301,59 @@
     head_count = grad_query.shape[1] * lax.axis_size("ctx") * HEAD_DIM
     query_blocks = query_cols // LANES
 
-    sizes, early = plan(pad(down_cols) // LANES)
+    sizes, groups = plan(pad(down_cols) // LANES)
     starts = [sum(sizes[:k]) for k in range(len(sizes))]
 
-    query_received = exchange(grad_query, query_rows, 0, query_blocks, me, [])
-    down_received = [exchange(grad_down, down_rows, starts[k], sizes[k], me, []) for k in range(min(2, len(sizes)))]
+    query_pieces = pieces_of(grad_query, query_rows, 0, query_blocks, me)
+    query_received = send(query_pieces, [])
+    pieces = [pieces_of(grad_down, down_rows, starts[k], sizes[k], me) for k in range(len(sizes))]
+    down_received = [send(pieces[0], [])]
 
     query_moment_new, query_sum = gather_moment(
         grad_query, query_received, query_moment, None, me, 0, query_blocks, replicas
     )
-    done = [query_sum]
+    if len(sizes) > 1:
+        down_received.append(send(pieces[1], [query_sum]))
     down_moment_new = None
-    down_sums = []
-    groups = [(0, early), (early, len(sizes) - 1), (len(sizes) - 1, len(sizes))]
-    groups = [g for g in groups if g[0] < g[1]]
-    seconds = []
-    chained = []
-    pending = None
+    down_sums, seconds, chained, waiting = [], [], [], []
     for k in range(len(sizes)):
-        if k + 2 < len(sizes):
-            down_received.append(exchange(grad_down, down_rows, starts[k + 2], sizes[k + 2], me, done))
         down_moment_new, squares = gather_moment(
             grad_down, down_received[k], down_moment, down_moment_new, me, starts[k], sizes[k], replicas
         )
         down_sums.append(squares)
         done = [squares]
-        for low, high in groups:
+        for number, (low, high) in enumerate(groups):
             if high != k + 1:
                 continue
+            width = sum(sizes[low:high]) * LANES
+            part = jnp.concatenate(down_sums[low:high], axis=1)
+            values, axes_of = [part], [("tensor",)]
+            if high == len(sizes):
+                axes_of = [("dp", "tensor")]
+            if low == 0:
+                values.append(query_sum)
+                axes_of.append(("dp", "ctx") if high == len(sizes) else ("ctx",))
+            totals = spread(values, axes_of, number)
+            done = [totals[0]]
+            joined = jnp.concatenate(totals, axis=1)
+            if high < len(sizes):
+                joined = total_over(joined, ("dp",))
+            waiting.append((joined, low, high, width))
+        ahead = k + 4 if k + 4 == len(sizes) else k + 3
+        while len(down_received) < min(ahead, len(sizes)):
+            down_received.append(send(pieces[len(down_received)], done))
+        while waiting and (k + 1 == len(sizes) or waiting[0][2] + (2 if waiting[0][1] else 1) <= k + 1):
+            joined, low, high, width = waiting.pop(0)
             begin = starts[low] * LANES
-            end = min(begin + sum(sizes[low:high]) * LANES, down_cols)
-            part = jnp.concatenate(down_sums[low:high], axis=1)
-            total = total_over(part, ("dp", "tensor"))
-            old = jnp.pad(down_second[begin:end], (0, part.shape[1] - (end - begin)))[None]
-            second = BETA_TWO * old + (1.0 - BETA_TWO) * (total / neuron_count)
+            end = min(begin + width, down_cols)
+            old = jnp.pad(down_second[begin:end], (0, width - (end - begin)))[None]
+            second = BETA_TWO * old + (1.0 - BETA_TWO) * (joined[:, :width] / neuron_count)
             seconds.append(second[0, : end - begin])
-            if pending is not None:
-                down_moment_new, *chained = finish(
-                    keep, pending[0], down_param, down_moment_new, chained, pending[1], pending[2]
-                )
-            pending = (second, starts[low], sum(sizes[low:high]))
+            down_moment_new, *chained = finish(
+                keep, second, down_param, down_moment_new, chained, starts[low], sum(sizes[low:high])
+            )
             if low == 0:
-                head_part = jnp.sum(query_sum.reshape(query_blocks, HEAD_DIM), axis=1)[None]
-                head_total = total_over(head_part, ("dp", "ctx"))[0]
+                head_total = jnp.sum(joined[0, width:].reshape(-1, HEAD_DIM), axis=1)
                 query_second_new = BETA_TWO * query_second + (1.0 - BETA_TWO) * (head_total / head_count)
                 query_moment_new, query_param_new, query_update = finish(
                     keep,
@@ -256,9 +364,6 @@
                     0,
                     query_blocks,
                 )
-    down_moment_new, *chained = finish(
-        keep, pending[0], down_param, down_moment_new, chained, pending[1], pending[2]
-    )
     down_param_new, down_update = chained
     return (
         down_param_new,
@@ -294,4 +399,5 @@
         P("tensor"),
         P(("ctx", "dp"), "tensor"),
     )
+
     return jax.shard_map(shards, mesh=mesh, in_specs=in_specs, out_specs=out_specs, check_vma=False)

time: 193 us -> 192 us (level)
  starting transfers between devices: 47.2 us -> 10.8 us
  Pallas kernels: 85.5 us -> 106 us
  waiting for transfers between devices: 49.3 us -> 57.8 us
  local copies, waits for them, and re-layouts: 4.87 us -> 8.34 us
  other arithmetic: 3.11 us -> 6.19 us
    ppermute x28 -> x2, starting transfers between devices: 35.1 us -> 2.03 us  [total_over(): lax.ppermute(value, axes, [(i, i ^ k) for i in range(size)])]
    pallas_call x0 -> x8, Pallas kernels: none -> 19.1 us  [the longest x3 19.1 us: spread(): pl.pallas_call(kernel, in_specs=[vmem] * number, out_specs=[vmem] * numbe...]
    ppermute x7, waiting for transfers between devices: 25.2 us -> 43.4 us  [send(): lax.ppermute(piece, 'dp', [(i, (i + d) % replicas) for i in range(replica...]
    ppermute x28 -> x2, waiting for transfers between devices: 24.1 us -> 14.4 us  [total_over(): lax.ppermute(value, axes, [(i, i ^ k) for i in range(size)])]
    unnamed x37 -> x33, local copies, waits for them, and re-layouts: 3.56 us -> 7.02 us
    ppermute x7, starting transfers between devices: 12.2 us -> 8.77 us  [send(): lax.ppermute(piece, 'dp', [(i, (i + d) % replicas) for i in range(replica...]
    concatenate x0 -> x2, other arithmetic: none -> 2.47 us  [shards(): part = jnp.concatenate(down_sums[low:high], axis=1)]
  transfers between devices with their start and end apart: 35 -> 9, of which waited for: 5 -> 4; matrix products, arithmetic and copies ran while one was open for 2% -> 3% of each run, Pallas kernels for 41% -> 44%
where the time goes in v2:
time: 192 us; the launch traced here: 190 us
  Pallas kernels  106 us (55%)
  waiting for transfers between devices  57.8 us (30%)
  starting transfers between devices  10.8 us (6%)
  local copies, waits for them, and re-layouts  8.34 us (4%)
  other arithmetic  6.19 us (3%)
    ppermute x7, waiting for transfers between devices, send(): lax.ppermute(piece, 'dp', [(i, (i + d) % replicas) for i in range(replica...  43.4 us
    pallas_call x7, Pallas kernels, gather_moment(): pl.pallas_call(kernel, grid_spec=pltpu.PrefetchScalarGridSpec(num_scalar_...  32.9 us
    pallas_call x4, Pallas kernels, finish(): pl.pallas_call(kernel, grid=(blocks, rows // tile), in_specs=[pl.BlockSpe...  29.2 us
    pallas_call x7, Pallas kernels, cut(): pl.pallas_call(kernel, grid_spec=pltpu.PrefetchScalarGridSpec(num_scalar_...  24.5 us
    pallas_call x3, Pallas kernels, spread(): pl.pallas_call(kernel, in_specs=[vmem] * number, out_specs=[vmem] * numbe...  19.1 us
    ppermute x2, waiting for transfers between devices, total_over(): lax.ppermute(value, axes, [(i, i ^ k) for i in range(size)])  14.4 us
    ppermute x7, starting transfers between devices, send(): lax.ppermute(piece, 'dp', [(i, (i + d) % replicas) for i in range(replica...  8.77 us
    unnamed x33, local copies, waits for them, and re-layouts  7.02 us
  transfers between devices with their start and end apart: 9, of which 4 were waited for; matrix products, arithmetic and copies ran while one was open for 3% of the time, Pallas kernels for 44%

profile of v2, /device:TPU:0, one launch (start us, length us, event | category | flops | bytes accessed | tf_op | source)
XLA Modules:
  0.0 190.4 jit_solution(14053628349637204875)
XLA Ops:
  0.6 4.4 %cut.8 = bf16[2304,256]{1,0:T(8,128)(2,1)} custom-call(s32[1]{0:T(128)} %bitcast.1.part_ref, bf16[1,4608,1152]{2,1,0:T(8,128)(2,1)} %grad_ref.27), custom_call_target="tpu_custom_call" | custom-call | bytes 2359296 | tf_op jit(solution)/shard_map/cut/pallas_call | solution.py:46
  5.0 3.0 %collective-permute-start = (bf16[2304,256]{1,0:T(8,128)(2,1)}, bf16[2304,256]{1,0:T(8,128)(2,1)S(1)}, u32[]{:S(2)}, u32[]{:S(2)}) collective-permute-start(bf16[2304,256]{1,0:T(8,128)(2,1)} %cut.8), channel_id=1, source_target_pairs={{0,16},{16,0},{1,17},{17,1},{2,18},{18,2},{3,19},{19,3},{4,20},{20... | collective-permute-start | bytes 3538952 | tf_op jit(solution)/shard_map/ppermute | solution.py:262
  8.0 3.2 %cut.10 = bf16[576,512]{1,0:T(8,128)(2,1)} custom-call(s32[1]{0:T(128)} %bitcast.1.part_ref, bf16[1,1152,512]{2,1,0:T(8,128)(2,1)} %grad_ref.19), custom_call_target="tpu_custom_call" | custom-call | bytes 1179648 | tf_op jit(solution)/shard_map/cut/pallas_call | solution.py:46
  11.2 4.4 %cut.9.refs_0_ = bf16[2304,256]{1,0:T(8,128)(2,1)} custom-call(s32[1]{0:T(128)} %bitcast.1.part_ref, bf16[1,4608,1152]{2,1,0:T(8,128)(2,1)} %grad_ref.27), custom_call_target="tpu_custom_call" | custom-call | bytes 2359296 | tf_op jit(solution)/shard_map/cut/pallas_call | solution.py:46
  15.6 31.3 %collective-permute-done.1.rest_0_ = bf16[576,512]{1,0:T(8,128)(2,1)S(1)} collective-permute-done((bf16[576,512]{1,0:T(8,128)(2,1)}, bf16[576,512]{1,0:T(8,128)(2,1)S(1)}, u32[]{:S(2)}, u32[]{:S(2)}) %collective-permute-start.1) | collective-permute-done | bytes 589856 | tf_op jit(solution)/shard_map/ppermute | solution.py:262
  47.7 3.9 %gather_moment.8 = (f32[576,512]{1,0:T(8,128)}, f32[1,512]{1,0:T(1,128)}) custom-call(s32[1]{0:T(128)} %bitcast.me_ref, bf16[1,1152,512]{2,1,0:T(8,128)(2,1)} %grad_ref.19, bf16[576,512]{1,0:T(8,128)(2,1)} %copy-done.3, f32[576,512]{1,0:T(8,128)} %rest_1_.8), custom_call_target="tpu_custom_call" | custom-call | bytes 3538944 | tf_op jit(solution)/shard_map/gather_moment/pallas_call | solution.py:88
  53.3 4.4 %cut.11.refs_0_ = bf16[2304,256]{1,0:T(8,128)(2,1)} custom-call(s32[1]{0:T(128)} %bitcast.1.part_ref, bf16[1,4608,1152]{2,1,0:T(8,128)(2,1)} %grad_ref.27), custom_call_target="tpu_custom_call" | custom-call | bytes 2359296 | tf_op jit(solution)/shard_map/cut/pallas_call | solution.py:46
  58.7 5.9 %gather_moment.7 = (f32[2304,1152]{1,0:T(8,128)}, f32[1,256]{1,0:T(1,128)}) custom-call(s32[1]{0:T(128)} %bitcast.me_ref, bf16[1,4608,1152]{2,1,0:T(8,128)(2,1)} %grad_ref.27, bf16[2304,256]{1,0:T(8,128)(2,1)} %copy-done.2, f32[2304,1152]{1,0:T(8,128)} %rest_1_.13), custom_call_target="tpu_custom_call" | custom-call | bytes 7077888 | tf_op jit(solution)/shard_map/gather_moment/pallas_call | solution.py:88
  65.0 2.8 %cut.7.refs_0_ = bf16[2304,128]{1,0:T(8,128)(2,1)} custom-call(s32[1]{0:T(128)} %bitcast.1.part_ref, bf16[1,4608,1152]{2,1,0:T(8,128)(2,1)} %grad_ref.27), custom_call_target="tpu_custom_call" | custom-call | bytes 1179648 | tf_op jit(solution)/shard_map/cut/pallas_call | solution.py:46
  68.5 12.1 %collective-permute-done.2.rest_0_ = bf16[2304,256]{1,0:T(8,128)(2,1)S(1)} collective-permute-done((bf16[2304,256]{1,0:T(8,128)(2,1)}, bf16[2304,256]{1,0:T(8,128)(2,1)S(1)}, u32[]{:S(2)}, u32[]{:S(2)}) %collective-permute-start.2) | collective-permute-done | bytes 1179680 | tf_op jit(solution)/shard_map/ppermute | solution.py:262
  81.7 5.9 %gather_moment.9 = (f32[2304,1152]{1,0:T(8,128)}, f32[1,256]{1,0:T(1,128)}) custom-call(s32[1]{0:T(128)} %bitcast.me_ref, bf16[1,4608,1152]{2,1,0:T(8,128)(2,1)} %grad_ref.27, bf16[2304,256]{1,0:T(8,128)(2,1)} %copy-done.1, f32[2304,1152]{1,0:T(8,128)} %rest_1_.13, f32[2304,1152]{1,0:T(8,128)} %get-tuple-element.38.rest_2_), custom_call_target="tpu_custom_call", output_to_operand_aliasing={{0}: (4, {})} | custom-call | bytes 7077888 | tf_op jit(solution)/shard_map/gather_moment/pallas_call | solution.py:88
  88.8 8.3 %spread.3 = (f32[1,512]{1,0:T(1,128)}, f32[1,512]{1,0:T(1,128)}) custom-call(f32[1,512]{1,0:T(1,128)} %pad_maximum_fusion.1.refs_0_, f32[1,512]{1,0:T(1,128)} %get-tuple-element.37.refs_1_), custom_call_target="tpu_custom_call" | custom-call | bytes 8000000 | tf_op jit(solution)/shard_map/spread/pallas_call | solution.py:221
  106.7 10.3 %collective-permute-done.4 = f32[1,1024]{1,0:T(1,128)S(1)} collective-permute-done((f32[1,1024]{1,0:T(1,128)S(1)}, f32[1,1024]{1,0:T(1,128)S(1)}, u32[]{:S(2)}, u32[]{:S(2)}) %collective-permute-start.4) | collective-permute-done | bytes 4128 | tf_op jit(solution)/shard_map/ppermute | solution.py:158
  118.0 5.9 %gather_moment.10 = (f32[2304,1152]{1,0:T(8,128)}, f32[1,256]{1,0:T(1,128)}) custom-call(s32[1]{0:T(128)} %bitcast.me_ref, bf16[1,4608,1152]{2,1,0:T(8,128)(2,1)} %grad_ref.27, bf16[2304,256]{1,0:T(8,128)(2,1)} %copy-done, f32[2304,1152]{1,0:T(8,128)} %rest_1_.13, f32[2304,1152]{1,0:T(8,128)} %get-tuple-element.42.rest_2_), custom_call_target="tpu_custom_call", output_to_operand_aliasing={{0}: (4, {})} | custom-call | bytes 7077888 | tf_op jit(solution)/shard_map/gather_moment/pallas_call | solution.py:88
  123.9 4.9 %spread.4.refs_1_ = f32[1,256]{1,0:T(1,128)} custom-call(f32[1,256]{1,0:T(1,128)} %get-tuple-element.46.refs_0_), custom_call_target="tpu_custom_call" | custom-call | bytes 8000000 | tf_op jit(solution)/shard_map/spread/pallas_call | solution.py:221
  133.7 3.9 %finish.7 = (f32[576,512]{1,0:T(8,128)}, f32[576,512]{1,0:T(8,128)}, bf16[576,512]{1,0:T(8,128)(2,1)}) custom-call(f32[2]{0:T(128)} %pad_maximum_fusion.3.keep_ref, f32[1,512]{1,0:T(1,128)} %bitcast.12, f32[576,512]{1,0:T(8,128)} %parameter_ref.7, f32[576,512]{1,0:T(8,128)} %get-tuple-element.60.moment_ref), custom_call_target="tpu_custom_call", output_to_operand_aliasing={{0}: (3, {})} | custom-call | bytes 4128768 | tf_op jit(solution)/shard_map/finish/pallas_call | solution.py:129
  137.6 10.7 %finish.4 = (f32[2304,1152]{1,0:T(8,128)}, f32[2304,1152]{1,0:T(8,128)}, bf16[2304,1152]{1,0:T(8,128)(2,1)}) custom-call(f32[2]{0:T(128)} %pad_maximum_fusion.3.keep_ref, f32[1,512]{1,0:T(1,128)} %get-tuple-element.67.second_ref, f32[2304,1152]{1,0:T(8,128)} %parameter_ref.6, f32[2304,1152]{1,0:T(8,128)} %get-tuple-element.43.moment_ref), custom_call_target="tpu_custom_call", output_to_operand_aliasing={{0}: (3, {})} | custom-call | bytes 16515072 | tf_op jit(solution)/shard_map/finish/pallas_call | solution.py:129
  149.2 3.7 %gather_moment.11 = (f32[2304,1152]{1,0:T(8,128)}, f32[1,128]{1,0:T(1,128)}) custom-call(s32[1]{0:T(128)} %bitcast.me_ref, bf16[1,4608,1152]{2,1,0:T(8,128)(2,1)} %grad_ref.27, bf16[2304,128]{1,0:T(8,128)(2,1)} %copy-done.4, f32[2304,1152]{1,0:T(8,128)} %rest_1_.13, f32[2304,1152]{1,0:T(8,128)} %get-tuple-element.44.rest_2_), custom_call_target="tpu_custom_call", output_to_operand_aliasing={{0}: (4, {})} | custom-call | bytes 3538944 | tf_op jit(solution)/shard_map/gather_moment/pallas_call | solution.py:88
  152.9 4.2 %collective-permute-done.8 = f32[1,256]{1,0:T(1,128)S(1)} collective-permute-done((f32[1,256]{1,0:T(1,128)}, f32[1,256]{1,0:T(1,128)S(1)}, u32[]{:S(2)}, u32[]{:S(2)}) %collective-permute-start.8) | collective-permute-done | bytes 1056 | tf_op jit(solution)/shard_map/ppermute | solution.py:158
  158.5 3.7 %gather_moment.12 = (f32[2304,1152]{1,0:T(8,128)}, f32[1,128]{1,0:T(1,128)}) custom-call(s32[1]{0:T(128)} %bitcast.me_ref, bf16[1,4608,1152]{2,1,0:T(8,128)(2,1)} %grad_ref.27, bf16[2304,128]{1,0:T(8,128)(2,1)} %copy-done.6, f32[2304,1152]{1,0:T(8,128)} %rest_1_.13, f32[2304,1152]{1,0:T(8,128)} %get-tuple-element.47.rest_2_), custom_call_target="tpu_custom_call", output_to_operand_aliasing={{0}: (4, {})} | custom-call | bytes 3538944 | tf_op jit(solution)/shard_map/gather_moment/pallas_call | solution.py:88
  162.3 5.8 %finish.5 = (f32[2304,1152]{1,0:T(8,128)}, f32[2304,1152]{1,0:T(8,128)}, bf16[2304,1152]{1,0:T(8,128)(2,1)}) custom-call(f32[2]{0:T(128)} %pad_maximum_fusion.3.keep_ref, f32[1,256]{1,0:T(1,128)} %multiply_add_fusion.1.second_ref, f32[2304,1152]{1,0:T(8,128)} %parameter_ref.6, ...), custom_call_target="tpu_custom_call", output_to_operand_aliasing={{0}: (3, {}), {1}: (4, {}), {2}: (5, {})} | custom-call | bytes 8257536 | tf_op jit(solution)/shard_map/finish/pallas_call | solution.py:129
  168.9 3.8 %gather_moment.13 = (f32[2304,1152]{1,0:T(8,128)}, f32[1,128]{1,0:T(1,128)}) custom-call(s32[1]{0:T(128)} %bitcast.me_ref, bf16[1,4608,1152]{2,1,0:T(8,128)(2,1)} %grad_ref.27, bf16[2304,128]{1,0:T(8,128)(2,1)} %copy-done.5, f32[2304,1152]{1,0:T(8,128)} %rest_1_.13, f32[2304,1152]{1,0:T(8,128)} %get-tuple-element.52.rest_2_), custom_call_target="tpu_custom_call", output_to_operand_aliasing={{0}: (4, {})} | custom-call | bytes 3538944 | tf_op jit(solution)/shard_map/gather_moment/pallas_call | solution.py:88
  173.9 5.9 %spread.5 = f32[1,384]{1,0:T(1,128)} custom-call(f32[1,384]{1,0:T(1,128)} %pad_maximum_fusion.2.refs_0_), custom_call_target="tpu_custom_call" | custom-call | bytes 8000000 | tf_op jit(solution)/shard_map/spread/pallas_call | solution.py:221
  181.6 8.8 %finish.6 = (f32[2304,1152]{1,0:T(8,128)}, f32[2304,1152]{1,0:T(8,128)}, bf16[2304,1152]{1,0:T(8,128)(2,1)}) custom-call(f32[2]{0:T(128)} %pad_maximum_fusion.3.keep_ref, f32[1,384]{1,0:T(1,128)} %get-tuple-element.65.second_ref, f32[2304,1152]{1,0:T(8,128)} %parameter_ref.6, ...), custom_call_target="tpu_custom_call", output_to_operand_aliasing={{0}: (3, {}), {1}: (4, {}), {2}: (5, {})} | custom-call | bytes 12386304 | tf_op jit(solution)/shard_map/finish/pallas_call | solution.py:129
  (68 shorter events, 27.8 us)
Async XLA Ops:
  5.0 52.7 %collective-permute-start = (bf16[2304,256]{1,0:T(8,128)(2,1)}, bf16[2304,256]{1,0:T(8,128)(2,1)S(1)}, u32[]{:S(2)}, u32[]{:S(2)}) collective-permute-start(bf16[2304,256]{1,0:T(8,128)(2,1)} %cut.8), channel_id=1, source_target_pairs={{0,16},{16,0},{1,17},{17,1},{2,18},{18,2},{3,19},{19,3},{4,20},{20... | collective-permute-start | bytes 3538952 | tf_op jit(solution)/shard_map/ppermute | solution.py:262
  11.2 35.6 %collective-permute-start.1 = (bf16[576,512]{1,0:T(8,128)(2,1)}, bf16[576,512]{1,0:T(8,128)(2,1)S(1)}, u32[]{:S(2)}, u32[]{:S(2)}) collective-permute-start(bf16[576,512]{1,0:T(8,128)(2,1)} %cut.10), channel_id=1, source_target_pairs={{0,16},{16,0},{1,17},{17,1},{2,18},{18,2},{3,19},{19,3},{4,20},{20... | collective-permute-start | bytes 1769480 | tf_op jit(solution)/shard_map/ppermute | solution.py:262
  51.6 29.0 %collective-permute-start.2 = (bf16[2304,256]{1,0:T(8,128)(2,1)}, bf16[2304,256]{1,0:T(8,128)(2,1)S(1)}, u32[]{:S(2)}, u32[]{:S(2)}) collective-permute-start(bf16[2304,256]{1,0:T(8,128)(2,1)} %held.5), channel_id=1, source_target_pairs={{0,16},{16,0},{1,17},{17,1},{2,18},{18,2},{3,19},{19,3},{4,20},{20... | collective-permute-start | bytes 3538952 | tf_op jit(solution)/shard_map/ppermute | solution.py:262
  57.7 1.0 copy-start.2
  64.6 3.8 %copy-start.11 = (f32[1152]{0:T(1024)S(1)}, f32[1152]{0:T(1024)}, u32[]{:S(2)}) copy-start(f32[1152]{0:T(1024)} %param.13) | copy-start | bytes 13828
  64.6 52.3 %collective-permute-start.5 = (bf16[2304,256]{1,0:T(8,128)(2,1)}, bf16[2304,256]{1,0:T(8,128)(2,1)S(1)}, u32[]{:S(2)}, u32[]{:S(2)}) collective-permute-start(bf16[2304,256]{1,0:T(8,128)(2,1)} %held.7), channel_id=1, source_target_pairs={{0,16},{16,0},{1,17},{17,1},{2,18},{18,2},{3,19},{19,3},{4,20},{20... | collective-permute-start | bytes 3538952 | tf_op jit(solution)/shard_map/ppermute | solution.py:262
  80.6 1.0 copy-start.1
  81.7 5.9 %copy-start.10 = (f32[1,256]{1,0:T(1,128)S(1)}, f32[1,256]{1,0:T(1,128)}, u32[]{:S(2)}) copy-start(f32[1,256]{1,0:T(1,128)} %get-tuple-element.36.refs_1_) | copy-start | bytes 3076
  97.2 51.2 %collective-permute-start.3 = (bf16[2304,128]{1,0:T(8,128)(2,1)}, bf16[2304,128]{1,0:T(8,128)(2,1)S(1)}, u32[]{:S(2)}, u32[]{:S(2)}) collective-permute-start(bf16[2304,128]{1,0:T(8,128)(2,1)} %held.6), channel_id=1, source_target_pairs={{0,16},{16,0},{1,17},{17,1},{2,18},{18,2},{3,19},{19,3},{4,20},{20... | collective-permute-start | bytes 1769480 | tf_op jit(solution)/shard_map/ppermute | solution.py:262
  100.1 16.8 %collective-permute-start.4 = (f32[1,1024]{1,0:T(1,128)S(1)}, f32[1,1024]{1,0:T(1,128)S(1)}, u32[]{:S(2)}, u32[]{:S(2)}) collective-permute-start(f32[1,1024]{1,0:T(1,128)S(1)} %constant_dynamic-update-slice_fusion), channel_id=1, source_target_pairs={{0,16},{16,0},{1,17},{17,1},{2,18},{18,2},{3,19},{19,3},{4,20},{20... | collective-permute-start | bytes 12296 | tf_op jit(solution)/shard_map/ppermute | solution.py:158
  117.0 1.0 copy-start
  118.0 15.1 %copy-start.15 = (f32[4]{0:T(128)S(1)}, f32[4]{0:T(128)}, u32[]{:S(2)}) copy-start(f32[4]{0:T(128)} %param.16) | copy-start | bytes 52
  128.8 28.9 %collective-permute-start.6 = (bf16[2304,128]{1,0:T(8,128)(2,1)}, bf16[2304,128]{1,0:T(8,128)(2,1)S(1)}, u32[]{:S(2)}, u32[]{:S(2)}) collective-permute-start(bf16[2304,128]{1,0:T(8,128)(2,1)} %held.8), channel_id=1, source_target_pairs={{0,16},{16,0},{1,17},{17,1},{2,18},{18,2},{3,19},{19,3},{4,20},{20... | collective-permute-start | bytes 1769480 | tf_op jit(solution)/shard_map/ppermute | solution.py:262
  130.3 37.8 %collective-permute-start.7 = (bf16[2304,128]{1,0:T(8,128)(2,1)}, bf16[2304,128]{1,0:T(8,128)(2,1)S(1)}, u32[]{:S(2)}, u32[]{:S(2)}) collective-permute-start(bf16[2304,128]{1,0:T(8,128)(2,1)} %held.9), channel_id=1, source_target_pairs={{0,16},{16,0},{1,17},{17,1},{2,18},{18,2},{3,19},{19,3},{4,20},{20... | collective-permute-start | bytes 1769480 | tf_op jit(solution)/shard_map/ppermute | solution.py:262
  131.6 25.5 %collective-permute-start.8 = (f32[1,256]{1,0:T(1,128)}, f32[1,256]{1,0:T(1,128)S(1)}, u32[]{:S(2)}, u32[]{:S(2)}) collective-permute-start(f32[1,256]{1,0:T(1,128)} %spread.4.refs_1_), channel_id=1, source_target_pairs={{0,16},{16,0},{1,17},{17,1},{2,18},{18,2},{3,19},{19,3},{4,20},{20... | collective-permute-start | bytes 3080 | tf_op jit(solution)/shard_map/ppermute | solution.py:158
  133.1 15.3 %copy-start.12 = (f32[4]{0:T(128)}, f32[4]{0:T(128)S(1)}, u32[]{:S(2)}) copy-start(f32[4]{0:T(128)S(1)} %multiply_add_fusion.2) | copy-start | bytes 52
  148.4 0.8 copy-start.4
  149.2 7.9 %copy-start.8 = (f32[1,256]{1,0:T(1,128)S(1)}, f32[1,256]{1,0:T(1,128)}, u32[]{:S(2)}) copy-start(f32[1,256]{1,0:T(1,128)} %spread.4.refs_1_) | copy-start | bytes 3076
  157.7 0.8 copy-start.6
  168.1 0.8 copy-start.5
  168.9 3.8 %copy-start.13 = (f32[1,128]{1,0:T(1,128)S(1)}, f32[1,128]{1,0:T(1,128)}, u32[]{:S(2)}) copy-start(f32[1,128]{1,0:T(1,128)} %get-tuple-element.45) | copy-start | bytes 1540
  168.9 3.8 %copy-start.14 = (f32[1,128]{1,0:T(1,128)S(1)}, f32[1,128]{1,0:T(1,128)}, u32[]{:S(2)}) copy-start(f32[1,128]{1,0:T(1,128)} %get-tuple-element.48) | copy-start | bytes 1540
  168.9 12.1 %copy-start.7 = (f32[1,512]{1,0:T(1,128)S(1)}, f32[1,512]{1,0:T(1,128)}, u32[]{:S(2)}) copy-start(f32[1,512]{1,0:T(1,128)} %get-tuple-element.67.second_ref) | copy-start | bytes 6148
  168.9 12.1 %copy-start.9 = (f32[1,256]{1,0:T(1,128)S(1)}, f32[1,256]{1,0:T(1,128)}, u32[]{:S(2)}) copy-start(f32[1,256]{1,0:T(1,128)} %multiply_add_fusion.1.second_ref) | copy-start | bytes 3076
  (1 other events, 0.8 us)
